TPU v7x, 32 devices: a whole 2x2x4 slice. The times are simulated.
32 devices in a mesh: rep: 2 (over x), dp: 16 (over y, z, core).
Axes of the slice: x: 2, y: 2, z: 4, core: 2. Of those that a mesh axis runs over, the one named last changes fastest.
Arguments:
- x: bfloat16 [32, 4096, 512], P(('rep', 'dp')), parts along dimension 0
- dy: bfloat16 [32, 4096, 512], P(('rep', 'dp')), parts along dimension 0
- w_gate: bfloat16 [2, 512, 2048], P(None, 'dp')
- w_up: bfloat16 [2, 512, 2048], P(None, 'dp')
- w_down: bfloat16 [2, 2048, 512], P(None, 'dp')
Outputs:
- output 1: bfloat16 [32, 4096, 512], P(('rep', 'dp')), parts along dimension 0
- output 2: bfloat16 [4, 512, 2048], P('rep', 'dp'), parts along dimension 0
- output 3: bfloat16 [4, 512, 2048], P('rep', 'dp'), parts along dimension 0
- output 4: bfloat16 [4, 2048, 512], P('rep', 'dp'), parts along dimension 0
There are 2 independent parts. A program takes and returns all parts, laid end to end along the dimension named above; an argument that names none is the same for every part.
All inputs are finite; a program needn't handle non-finite values.
Results may differ from a plain program's by a relative error of at most 0.018.
Values are sent between devices in bfloat16 or wider.
A program may use at most 2 GiB of HBM per device.

v0:
```python
import jax
import jax.numpy as jnp
from jax import lax

NAMES = ("w_gate", "w_up", "w_down")


def matmul(a, w):
    return jnp.dot(a, w, preferred_element_type=jnp.float32).astype(jnp.bfloat16)


def normed(h):
    wide = h.astype(jnp.float32)
    scale = lax.rsqrt(jnp.mean(wide**2, -1, keepdims=True) + 1e-6)
    return (wide * scale).astype(jnp.bfloat16)


def layer(h, w):
    a = normed(h)
    gate = jnp.dot(a, w["w_gate"], preferred_element_type=jnp.float32)
    up = jnp.dot(a, w["w_up"], preferred_element_type=jnp.float32)
    return h + matmul((jax.nn.silu(gate) * up).astype(jnp.bfloat16), w["w_down"])


def stack(weights, h):
    for number in range(weights["w_gate"].shape[0]):
        h = layer(h, {name: w[number] for name, w in weights.items()})
    return h


def solution(mesh):
    groups = mesh.shape["rep"]

    def step(x, dy, *weights):
        shape = x.shape
        x, dy = (t.reshape(groups, -1, *t.shape[1:]) for t in (x, dy))

        def of_a_group(x, dy):
            _, back = jax.vjp(stack, dict(zip(NAMES, weights, strict=True)), x)
            by_weights, by_x = back(dy)
            return (by_x, *(by_weights[name] for name in NAMES))

        by_x, *by_weights = jax.vmap(of_a_group)(x, dy)
        return (by_x.reshape(shape), *(t.reshape(-1, *t.shape[2:]) for t in by_weights))

    return step
```

profile of v0, /device:TPU:0, one launch (start us, length us, event | category | flops | bytes accessed | tf_op | source)
XLA Modules:
  0.0 1194.0 jit_solution(5955806994804325624)
XLA Ops:
  37.3 17.4 %all-gather.30.cloned.1.call-done = bf16[1,512,2048]{2,1,0:T(8,128)(2,1)} async-done(((bf16[1,32,2048]{2,1,0:T(8,128)(2,1)}), bf16[1,512,2048]{2,1,0:T(8,128)(2,1)}) %all-gather.30.cloned.1.call-update) | async-done | bytes 2097168 | tf_op jit(solution)/vmap(jvp())/squeeze | solution.py:27
  54.7 17.8 %fusion.239 = f32[4096,2048]{1,0:T(8,128)} fusion(bf16[1,512,2048]{2,1,0:T(8,128)(2,1)} %all-gather.30.cloned.1.call-done, bf16[1,4096,512]{2,1,0:T(8,128)(2,1)} %param.13, f32[4096]{0:T(1024)S(1)} %get-tuple-element.267), kind=kOutput, calls=%fused_computation.260 | convolution fusion | flops 8596226048 | bytes 39862272 | tf_op jit(solution)/vmap(jvp())/dot_general | solution.py:20
  72.5 24.6 %all-gather.32.cloned.1.call-done = bf16[1,512,2048]{2,1,0:T(8,128)(2,1)} async-done(((bf16[1,32,2048]{2,1,0:T(8,128)(2,1)}), bf16[1,512,2048]{2,1,0:T(8,128)(2,1)}) %all-gather.32.cloned.1.call-update) | async-done | bytes 2097168 | tf_op jit(solution)/vmap(jvp())/squeeze | solution.py:27
  97.2 31.8 %fusion.168 = (bf16[1,1,4096,2048]{3,2,1,0:T(8,128)(2,1)}, f32[4096,2048]{1,0:T(8,128)}) fusion(f32[4096,2048]{1,0:T(8,128)} %fusion.239, bf16[1,512,2048]{2,1,0:T(8,128)(2,1)} %all-gather.32.cloned.1.call-done, bf16[1,4096,512]{2,1,0:T(8,128)(2,1)} %param.13, f32[4096]{0:T(1024)S(1)} %get-tuple-element.267), kind=kOutput, calls=%fused_computation.195 | convolution fusion | flops 8646557696 | bytes 90193920 | tf_op jit(solution)/vmap(jvp())/dot_general | solution.py:21
  129.0 10.7 all-gather.34.cloned.1.call-done
  139.6 16.3 %fusion.182 = (f32[4096]{0:T(1024)S(1)}, bf16[1,1,4096,512]{2,3,1,0:T(8,128)(2,1)}) fusion(bf16[1,2048,512]{2,1,0:T(8,128)(2,1)} %all-gather.34.cloned.1.call-done, bf16[1,1,4096,2048]{3,2,1,0:T(8,128)(2,1)} %get-tuple-element.268, bf16[1,4096,512]{1,2,0:T(8,128)(2,1)} %copy.1), kind=kOutput, calls=%fused_computation.225 | convolution fusion | flops 8600416256 | bytes 27279360 | tf_op jit(solution)/vmap(jvp())/dot_general | solution.py:9
  162.5 21.1 %copy.4 = bf16[1,1,4096,2048]{2,3,1,0:T(8,128)(2,1)} copy(bf16[1,1,4096,2048]{3,2,1,0:T(8,128)(2,1)} %get-tuple-element.268) | data formatting | bytes 33554432
  183.6 14.9 %convolution_convert_fusion.1 = bf16[4096,2048]{1,0:T(8,128)(2,1)} fusion(bf16[1,4096,512]{2,1,0:T(8,128)(2,1)} %param.12, bf16[1,2048,512]{2,1,0:T(8,128)(2,1)} %all-gather.38.cloned.1.call-done), kind=kOutput, calls=%fused_computation.205 | convolution fusion | flops 8598323200 | bytes 23068672 | tf_op jit(solution)/vmap(transpose(jvp()))/dot_general | solution.py:9
  198.5 25.8 %all-gather.40.cloned.1.call-done = bf16[1,512,2048]{2,1,0:T(8,128)(2,1)} async-done(((bf16[1,32,2048]{2,1,0:T(8,128)(2,1)}), bf16[1,512,2048]{2,1,0:T(8,128)(2,1)}) %all-gather.40.cloned.1.call-update) | async-done | bytes 2097168 | tf_op jit(solution)/vmap(jvp())/squeeze | solution.py:27
  224.3 18.1 %fusion.224 = f32[4096,2048]{1,0:T(8,128)} fusion(bf16[1,1,4096,512]{2,3,1,0:T(8,128)(2,1)} %fusion.183, bf16[1,512,2048]{2,1,0:T(8,128)(2,1)} %all-gather.40.cloned.1.call-done), kind=kOutput, calls=%fused_computation.245 | convolution fusion | flops 8589934592 | bytes 39845888 | tf_op jit(solution)/vmap(jvp())/dot_general | solution.py:21
  242.4 24.3 %all-gather.36.cloned.1.call-done = bf16[1,512,2048]{2,1,0:T(8,128)(2,1)} async-done(((bf16[1,32,2048]{2,1,0:T(8,128)(2,1)}), bf16[1,512,2048]{2,1,0:T(8,128)(2,1)}) %all-gather.36.cloned.1.call-update) | async-done | bytes 2097168 | tf_op jit(solution)/vmap(jvp())/squeeze | solution.py:27
  266.7 44.6 %fusion.153 = (bf16[1,1,4096,2048]{3,2,1,0:T(8,128)(2,1)}, bf16[1,1,4096,2048]{3,2,1,0:T(8,128)(2,1)}, f32[4096,2048]{1,0:T(8,128)}) fusion(f32[4096,2048]{1,0:T(8,128)} %fusion.224, bf16[4096,2048]{1,0:T(8,128)(2,1)} %convolution_convert_fusion.1, bf16[1,512,2048]{2,1,0:T(8,128)(2,1)} %all-gather.36.cloned.1.call-done, bf16[1,1,4096,512]{2,3,1,0:T(8,128)(2,1)} %fusion.183), kind=kOutput, calls=%fused_computation.175 | convolution fusion | flops 8715763712 | bytes 123731968 | tf_op jit(solution)/vmap(jvp())/dot_general | solution.py:20
  311.3 27.6 %fusion.162 = bf16[1,1,4096,2048]{3,2,1,0:T(8,128)(2,1)} fusion(f32[4096,2048]{1,0:T(8,128)} %fusion.224, f32[4096,2048]{1,0:T(8,128)} %get-tuple-element.272), kind=kLoop, calls=%fused_computation.185 | loop fusion | flops 50331648 | bytes 83886080 | tf_op jit(solution)/vmap(jvp())/convert_element_type | solution.py:22
  338.9 21.4 %copy.2 = bf16[1,1,4096,2048]{2,3,1,0:T(8,128)(2,1)} copy(bf16[1,1,4096,2048]{3,2,1,0:T(8,128)(2,1)} %fusion.162) | data formatting | bytes 33554432
  360.3 93.7 %while.16 = (bf16[1,1,4096,2048]{2,3,1,0:T(8,128)(2,1)}, bf16[1,1,4096,512]{3,2,1,0:T(8,128)(2,1)}, f32[1,128,512]{2,1,0:T(8,128)S(1)}, f32[1,128,512]{2,1,0:T(8...) while((bf16[1,1,4096,2048]{2,3,1,0:T(8,128)(2,1)}, ...), condition=%wide.windowed_dot_general_cond_rs.4.clone, body=%wide.windowed_dot_general_body_rs.4.clone.sunk | while | flops 2156265472 | bytes 135266992 | solution.py:9
  454.0 14.5 %fusion.188 = bf16[4096,512]{0,1:T(8,128)(2,1)} fusion(bf16[1,1,4096,2048]{3,2,1,0:T(8,128)(2,1)} %get-tuple-element.628, bf16[1,512,2048]{2,1,0:T(8,128)(2,1)S(1)} %copy-done.33), kind=kOutput, calls=%fused_computation.229 | convolution fusion | flops 8589934592 | bytes 23068672 | tf_op jit(solution)/vmap(transpose(jvp()))/dot_general | solution.py:21
  468.5 16.8 %fusion.184 = (f32[4096]{0:T(1024)S(1)}, bf16[1,1,4096,512]{2,3,1,0:T(8,128)(2,1)S(1)}) fusion(bf16[1,1,4096,512]{2,3,1,0:T(8,128)(2,1)S(1)} %copy-done.6, bf16[4096,512]{0,1:T(8,128)(2,1)} %fusion.188, bf16[1,512,2048]{2,1,0:T(8,128)(2,1)} %all-gather.36.cloned.1.call-done, bf16[1,1,4096,2048]{3,2,1,0:T(8,128)(2,1)} %get-tuple-element.550), kind=kOutput, calls=%fused_computation.227 | convolution fusion | flops 8600416256 | bytes 31473664 | tf_op jit(solution)/vmap(transpose(jvp()))/dot_general | solution.py:20
  496.2 94.4 %while.17 = (bf16[1,1,4096,2048]{2,3,1,0:T(8,128)(2,1)}, bf16[1,1,4096,512]{3,2,1,0:T(8,128)(2,1)}, f32[1,128,512]{2,1,0:T(8,128)S(1)}, f32[1,128,512]{2,1,0:T(8...) while((bf16[1,1,4096,2048]{2,3,1,0:T(8,128)(2,1)}, ...), condition=%wide.windowed_dot_general_cond_rs.5.clone, body=%wide.windowed_dot_general_body_rs.5.clone.sunk | while | flops 2156265472 | bytes 135266992 | solution.py:9
  591.4 125.2 %while.14 = (bf16[1,1,4096,512]{2,3,1,0:T(8,128)(2,1)}, bf16[1,1,4096,2048]{3,2,1,0:T(8,128)(2,1)}, f32[1,32,2048]{2,1,0:T(8,128)S(1)}, f32[1,32,2048]{2,1,0:T(8...) while((bf16[1,1,4096,512]{2,3,1,0:T(8,128)(2,1)}, ...), condition=%wide.windowed_dot_general_cond_rs.2.clone, body=%wide.windowed_dot_general_body_rs.2.clone.sunk | while | flops 2149974016 | bytes 51380836 | solution.py:21
  661.1 9.0 fusion.321
  716.5 40.7 %fusion.155 = (bf16[1,1,4096,2048]{3,2,1,0:T(8,128)(2,1)}, bf16[1,1,4096,2048]{3,2,1,0:T(8,128)(2,1)}) fusion(f32[4096,2048]{1,0:T(8,128)} %fusion.239, f32[4096,2048]{1,0:T(8,128)} %get-tuple-element.269, bf16[1,2048,512]{2,1,0:T(8,128)(2,1)} %all-gather.34.cloned.1.call-done, bf16[1,1,4096,512]{2,3,1,0:T(8,128)(2,1)} %fusion.220), kind=kOutput, calls=%fused_computation.177 | convolution fusion | flops 8724152320 | bytes 106954752 | tf_op jit(solution)/vmap(transpose(jvp()))/dot_general | solution.py:9
  757.3 13.9 %fusion.194 = bf16[4096,512]{0,1:T(8,128)(2,1)} fusion(bf16[1,1,4096,2048]{3,2,1,0:T(8,128)(2,1)} %get-tuple-element.589, bf16[1,512,2048]{2,1,0:T(8,128)(2,1)S(1)} %copy-done.32), kind=kOutput, calls=%fused_computation.231 | convolution fusion | flops 8589934592 | bytes 23068672 | tf_op jit(solution)/vmap(transpose(jvp()))/dot_general | solution.py:21
  771.2 31.2 %fusion.181 = (bf16[1,1,4096,512]{2,3,1,0:T(8,128)(2,1)}, f32[4096]{0:T(1024)}, bf16[1,1,4096,512]{2,3,1,0:T(8,128)(2,1)}) fusion(bf16[1,4096,512]{1,2,0:T(8,128)(2,1)S(1)} %copy-done.5, f32[4096]{0:T(1024)S(1)} %bitcast.594, bf16[4096,512]{0,1:T(8,128)(2,1)} %fusion.194, bf16[1,512,2048]{2,1,0:T(8,128)(2,1)S(1)} %copy-done.31, ...), kind=kOutput, calls=%fused_computation.224 | convolution fusion | flops 8604610560 | bytes 35684352 | tf_op jit(solution)/vmap(transpose(jvp()))/dot_general | solution.py:20
  802.5 119.2 %while.15 = (bf16[1,1,4096,512]{2,3,1,0:T(8,128)(2,1)}, bf16[1,1,4096,2048]{3,2,1,0:T(8,128)(2,1)}, f32[1,32,2048]{2,1,0:T(8,128)S(1)}, f32[1,32,2048]{2,1,0:T(8...) while((bf16[1,1,4096,512]{2,3,1,0:T(8,128)(2,1)}, ...), condition=%wide.windowed_dot_general_cond_rs.3.clone, body=%wide.windowed_dot_general_body_rs.3.clone.sunk | while | flops 2149974016 | bytes 51380836 | solution.py:21
  868.6 9.0 fusion.329
  898.4 9.0 fusion.329
  921.8 119.4 %while.12 = (bf16[1,1,4096,512]{2,3,1,0:T(8,128)(2,1)}, bf16[1,1,4096,2048]{3,2,1,0:T(8,128)(2,1)}, f32[1,32,2048]{2,1,0:T(8,128)S(1)}, f32[1,32,2048]{2,1,0:T(8...) while((bf16[1,1,4096,512]{2,3,1,0:T(8,128)(2,1)}, ...), condition=%wide.windowed_dot_general_cond_rs.clone, body=%wide.windowed_dot_general_body_rs.clone.sunk | while | flops 2149974016 | bytes 51380836 | solution.py:20
  988.1 9.0 fusion.305
  1041.3 119.2 %while.13 = (bf16[1,1,4096,512]{2,3,1,0:T(8,128)(2,1)}, bf16[1,1,4096,2048]{3,2,1,0:T(8,128)(2,1)}, f32[1,32,2048]{2,1,0:T(8,128)S(1)}, f32[1,32,2048]{2,1,0:T(8...) while((bf16[1,1,4096,512]{2,3,1,0:T(8,128)(2,1)}, ...), condition=%wide.windowed_dot_general_cond_rs.1.clone, body=%wide.windowed_dot_general_body_rs.1.clone.sunk | while | flops 2149974016 | bytes 51380836 | solution.py:20
  1047.8 9.0 fusion.313
  1107.4 9.0 fusion.313
  1137.2 9.0 fusion.313
  (511 shorter events, 633.5 us)
Async XLA Ops:
  7.2 47.5 %all-gather.30.cloned.1.call-start = ((), (), s32[]{:S(2)}) async-start(), calls=%async_computation | async-start | bytes 2228224 | tf_op jit(solution)/vmap(jvp())/squeeze | solution.py:27
  8.9 88.2 %all-gather.32.cloned.1.call-start = ((), (), s32[]{:S(2)}) async-start(), calls=%async_computation.1 | async-start | bytes 2228224 | tf_op jit(solution)/vmap(jvp())/squeeze | solution.py:27
  10.7 128.9 %all-gather.34.cloned.1.call-start = ((), (), s32[]{:S(2)}) async-start(), calls=%async_computation.2 | async-start | bytes 2228224 | tf_op jit(solution)/vmap(jvp())/squeeze | solution.py:27
  12.5 171.1 %all-gather.38.cloned.1.call-start = ((), (), s32[]{:S(2)}) async-start(), calls=%async_computation.4 | async-start | bytes 2228224 | tf_op jit(solution)/vmap(jvp())/squeeze | solution.py:27
  13.1 211.2 %all-gather.40.cloned.1.call-start = ((), (), s32[]{:S(2)}) async-start(), calls=%async_computation.5 | async-start | bytes 2228224 | tf_op jit(solution)/vmap(jvp())/squeeze | solution.py:27
  13.7 253.0 %all-gather.36.cloned.1.call-start = ((), (), s32[]{:S(2)}) async-start(), calls=%async_computation.3 | async-start | bytes 2228224 | tf_op jit(solution)/vmap(jvp())/squeeze | solution.py:27
  454.0 721.8 %collective-permute-start.28 = (f32[1,128,512]{2,1,0:T(8,128)}, f32[1,128,512]{2,1,0:T(8,128)}, u32[]{:S(2)}, u32[]{:S(2)}) collective-permute-start(f32[1,128,512]{2,1,0:T(8,128)} %get-tuple-element.45), channel_id=42, source_target_pairs={{0,1},{1,2},{2,3},{3,4},{4,5},{5,6},{6,7},{7,8},{8,9},{9,10},{10,1... | collective-permute-start | bytes 786440 | tf_op jit(solution)/vmap(transpose(jvp()))/dot_general | solution.py:9
  590.6 586.1 %collective-permute-start.29 = (f32[1,128,512]{2,1,0:T(8,128)}, f32[1,128,512]{2,1,0:T(8,128)}, u32[]{:S(2)}, u32[]{:S(2)}) collective-permute-start(f32[1,128,512]{2,1,0:T(8,128)} %get-tuple-element.47), channel_id=48, source_target_pairs={{0,1},{1,2},{2,3},{3,4},{4,5},{5,6},{6,7},{7,8},{8,9},{9,10},{10,1... | collective-permute-start | bytes 786440 | tf_op jit(solution)/vmap(transpose(jvp()))/dot_general | solution.py:9
  591.6 16.3 %collective-permute-start.8 = (f32[1,32,2048]{2,1,0:T(8,128)S(1)}, f32[1,32,2048]{2,1,0:T(8,128)S(1)}, u32[]{:S(2)}, u32[]{:S(2)}) collective-permute-start(f32[1,32,2048]{2,1,0:T(8,128)S(1)} %broadcast_select_fusion.28), channel_id=27, source_target_pairs={{0,1},{1,2},{2,3},{3,4},{4,5},{5,6},{6,7},{7,8},{8,9},{9,10},{10,1... | collective-permute-start | bytes 786440 | tf_op jit(solution)/vmap(transpose(jvp()))/dot_general | solution.py:21
  591.6 16.2 %collective-permute-start.9 = (f32[1,32,2048]{2,1,0:T(8,128)S(1)}, f32[1,32,2048]{2,1,0:T(8,128)S(1)}, u32[]{:S(2)}, u32[]{:S(2)}) collective-permute-start(f32[1,32,2048]{2,1,0:T(8,128)S(1)} %broadcast_select_fusion.29), channel_id=26, source_target_pairs={{0,15},{1,0},{2,1},{3,2},{4,3},{5,4},{6,5},{7,6},{8,7},{9,8},{10,9... | collective-permute-start | bytes 786440 | tf_op jit(solution)/vmap(transpose(jvp()))/dot_general | solution.py:21
  623.2 16.1 %collective-permute-start.8 = (f32[1,32,2048]{2,1,0:T(8,128)S(1)}, f32[1,32,2048]{2,1,0:T(8,128)S(1)}, u32[]{:S(2)}, u32[]{:S(2)}) collective-permute-start(f32[1,32,2048]{2,1,0:T(8,128)S(1)} %broadcast_select_fusion.28), channel_id=27, source_target_pairs={{0,1},{1,2},{2,3},{3,4},{4,5},{5,6},{6,7},{7,8},{8,9},{9,10},{10,1... | collective-permute-start | bytes 786440 | tf_op jit(solution)/vmap(transpose(jvp()))/dot_general | solution.py:21
  654.6 16.1 %collective-permute-start.8 = (f32[1,32,2048]{2,1,0:T(8,128)S(1)}, f32[1,32,2048]{2,1,0:T(8,128)S(1)}, u32[]{:S(2)}, u32[]{:S(2)}) collective-permute-start(f32[1,32,2048]{2,1,0:T(8,128)S(1)} %broadcast_select_fusion.28), channel_id=27, source_target_pairs={{0,1},{1,2},{2,3},{3,4},{4,5},{5,6},{6,7},{7,8},{8,9},{9,10},{10,1... | collective-permute-start | bytes 786440 | tf_op jit(solution)/vmap(transpose(jvp()))/dot_general | solution.py:21
  654.7 16.0 %collective-permute-start.9 = (f32[1,32,2048]{2,1,0:T(8,128)S(1)}, f32[1,32,2048]{2,1,0:T(8,128)S(1)}, u32[]{:S(2)}, u32[]{:S(2)}) collective-permute-start(f32[1,32,2048]{2,1,0:T(8,128)S(1)} %broadcast_select_fusion.29), channel_id=26, source_target_pairs={{0,15},{1,0},{2,1},{3,2},{4,3},{5,4},{6,5},{7,6},{8,7},{9,8},{10,9... | collective-permute-start | bytes 786440 | tf_op jit(solution)/vmap(transpose(jvp()))/dot_general | solution.py:21
  686.1 16.1 %collective-permute-start.8 = (f32[1,32,2048]{2,1,0:T(8,128)S(1)}, f32[1,32,2048]{2,1,0:T(8,128)S(1)}, u32[]{:S(2)}, u32[]{:S(2)}) collective-permute-start(f32[1,32,2048]{2,1,0:T(8,128)S(1)} %broadcast_select_fusion.28), channel_id=27, source_target_pairs={{0,1},{1,2},{2,3},{3,4},{4,5},{5,6},{6,7},{7,8},{8,9},{9,10},{10,1... | collective-permute-start | bytes 786440 | tf_op jit(solution)/vmap(transpose(jvp()))/dot_general | solution.py:21
  716.5 458.1 %collective-permute-start.26 = (f32[1,32,2048]{2,1,0:T(8,128)}, f32[1,32,2048]{2,1,0:T(8,128)}, u32[]{:S(2)}, u32[]{:S(2)}) collective-permute-start(f32[1,32,2048]{2,1,0:T(8,128)} %get-tuple-element.41), channel_id=30, source_target_pairs={{0,1},{1,2},{2,3},{3,4},{4,5},{5,6},{6,7},{7,8},{8,9},{9,10},{10,1... | collective-permute-start | bytes 786440 | tf_op jit(solution)/vmap(transpose(jvp()))/dot_general | solution.py:21
  802.5 16.1 %collective-permute-start.12 = (f32[1,32,2048]{2,1,0:T(8,128)S(1)}, f32[1,32,2048]{2,1,0:T(8,128)S(1)}, u32[]{:S(2)}, u32[]{:S(2)}) collective-permute-start(f32[1,32,2048]{2,1,0:T(8,128)S(1)} %broadcast_select_fusion.30), channel_id=33, source_target_pairs={{0,1},{1,2},{2,3},{3,4},{4,5},{5,6},{6,7},{7,8},{8,9},{9,10},{10,1... | collective-permute-start | bytes 786440 | tf_op jit(solution)/vmap(transpose(jvp()))/dot_general | solution.py:21
  802.6 16.0 %collective-permute-start.13 = (f32[1,32,2048]{2,1,0:T(8,128)S(1)}, f32[1,32,2048]{2,1,0:T(8,128)S(1)}, u32[]{:S(2)}, u32[]{:S(2)}) collective-permute-start(f32[1,32,2048]{2,1,0:T(8,128)S(1)} %broadcast_select_fusion.31), channel_id=32, source_target_pairs={{0,15},{1,0},{2,1},{3,2},{4,3},{5,4},{6,5},{7,6},{8,7},{9,8},{10,9... | collective-permute-start | bytes 786440 | tf_op jit(solution)/vmap(transpose(jvp()))/dot_general | solution.py:21
  832.4 16.1 %collective-permute-start.12 = (f32[1,32,2048]{2,1,0:T(8,128)S(1)}, f32[1,32,2048]{2,1,0:T(8,128)S(1)}, u32[]{:S(2)}, u32[]{:S(2)}) collective-permute-start(f32[1,32,2048]{2,1,0:T(8,128)S(1)} %broadcast_select_fusion.30), channel_id=33, source_target_pairs={{0,1},{1,2},{2,3},{3,4},{4,5},{5,6},{6,7},{7,8},{8,9},{9,10},{10,1... | collective-permute-start | bytes 786440 | tf_op jit(solution)/vmap(transpose(jvp()))/dot_general | solution.py:21
  862.2 16.1 %collective-permute-start.12 = (f32[1,32,2048]{2,1,0:T(8,128)S(1)}, f32[1,32,2048]{2,1,0:T(8,128)S(1)}, u32[]{:S(2)}, u32[]{:S(2)}) collective-permute-start(f32[1,32,2048]{2,1,0:T(8,128)S(1)} %broadcast_select_fusion.30), channel_id=33, source_target_pairs={{0,1},{1,2},{2,3},{3,4},{4,5},{5,6},{6,7},{7,8},{8,9},{9,10},{10,1... | collective-permute-start | bytes 786440 | tf_op jit(solution)/vmap(transpose(jvp()))/dot_general | solution.py:21
  862.2 16.0 %collective-permute-start.13 = (f32[1,32,2048]{2,1,0:T(8,128)S(1)}, f32[1,32,2048]{2,1,0:T(8,128)S(1)}, u32[]{:S(2)}, u32[]{:S(2)}) collective-permute-start(f32[1,32,2048]{2,1,0:T(8,128)S(1)} %broadcast_select_fusion.31), channel_id=32, source_target_pairs={{0,15},{1,0},{2,1},{3,2},{4,3},{5,4},{6,5},{7,6},{8,7},{9,8},{10,9... | collective-permute-start | bytes 786440 | tf_op jit(solution)/vmap(transpose(jvp()))/dot_general | solution.py:21
  892.0 16.1 %collective-permute-start.12 = (f32[1,32,2048]{2,1,0:T(8,128)S(1)}, f32[1,32,2048]{2,1,0:T(8,128)S(1)}, u32[]{:S(2)}, u32[]{:S(2)}) collective-permute-start(f32[1,32,2048]{2,1,0:T(8,128)S(1)} %broadcast_select_fusion.30), channel_id=33, source_target_pairs={{0,1},{1,2},{2,3},{3,4},{4,5},{5,6},{6,7},{7,8},{8,9},{9,10},{10,1... | collective-permute-start | bytes 786440 | tf_op jit(solution)/vmap(transpose(jvp()))/dot_general | solution.py:21
  922.0 16.1 %collective-permute-start = (f32[1,32,2048]{2,1,0:T(8,128)S(1)}, f32[1,32,2048]{2,1,0:T(8,128)S(1)}, u32[]{:S(2)}, u32[]{:S(2)}) collective-permute-start(f32[1,32,2048]{2,1,0:T(8,128)S(1)} %broadcast_select_fusion.24), channel_id=15, source_target_pairs={{0,1},{1,2},{2,3},{3,4},{4,5},{5,6},{6,7},{7,8},{8,9},{9,10},{10,1... | collective-permute-start | bytes 786440 | tf_op jit(solution)/vmap(transpose(jvp()))/dot_general | solution.py:20
  951.8 16.1 %collective-permute-start = (f32[1,32,2048]{2,1,0:T(8,128)S(1)}, f32[1,32,2048]{2,1,0:T(8,128)S(1)}, u32[]{:S(2)}, u32[]{:S(2)}) collective-permute-start(f32[1,32,2048]{2,1,0:T(8,128)S(1)} %broadcast_select_fusion.24), channel_id=15, source_target_pairs={{0,1},{1,2},{2,3},{3,4},{4,5},{5,6},{6,7},{7,8},{8,9},{9,10},{10,1... | collective-permute-start | bytes 786440 | tf_op jit(solution)/vmap(transpose(jvp()))/dot_general | solution.py:20
  981.6 16.1 %collective-permute-start = (f32[1,32,2048]{2,1,0:T(8,128)S(1)}, f32[1,32,2048]{2,1,0:T(8,128)S(1)}, u32[]{:S(2)}, u32[]{:S(2)}) collective-permute-start(f32[1,32,2048]{2,1,0:T(8,128)S(1)} %broadcast_select_fusion.24), channel_id=15, source_target_pairs={{0,1},{1,2},{2,3},{3,4},{4,5},{5,6},{6,7},{7,8},{8,9},{9,10},{10,1... | collective-permute-start | bytes 786440 | tf_op jit(solution)/vmap(transpose(jvp()))/dot_general | solution.py:20
  981.7 16.0 %collective-permute-start.1 = (f32[1,32,2048]{2,1,0:T(8,128)S(1)}, f32[1,32,2048]{2,1,0:T(8,128)S(1)}, u32[]{:S(2)}, u32[]{:S(2)}) collective-permute-start(f32[1,32,2048]{2,1,0:T(8,128)S(1)} %broadcast_select_fusion.25), channel_id=14, source_target_pairs={{0,15},{1,0},{2,1},{3,2},{4,3},{5,4},{6,5},{7,6},{8,7},{9,8},{10,9... | collective-permute-start | bytes 786440 | tf_op jit(solution)/vmap(transpose(jvp()))/dot_general | solution.py:20
  1011.4 16.1 %collective-permute-start = (f32[1,32,2048]{2,1,0:T(8,128)S(1)}, f32[1,32,2048]{2,1,0:T(8,128)S(1)}, u32[]{:S(2)}, u32[]{:S(2)}) collective-permute-start(f32[1,32,2048]{2,1,0:T(8,128)S(1)} %broadcast_select_fusion.24), channel_id=15, source_target_pairs={{0,1},{1,2},{2,3},{3,4},{4,5},{5,6},{6,7},{7,8},{8,9},{9,10},{10,1... | collective-permute-start | bytes 786440 | tf_op jit(solution)/vmap(transpose(jvp()))/dot_general | solution.py:20
  1041.3 16.1 %collective-permute-start.4 = (f32[1,32,2048]{2,1,0:T(8,128)S(1)}, f32[1,32,2048]{2,1,0:T(8,128)S(1)}, u32[]{:S(2)}, u32[]{:S(2)}) collective-permute-start(f32[1,32,2048]{2,1,0:T(8,128)S(1)} %broadcast_select_fusion.26), channel_id=21, source_target_pairs={{0,1},{1,2},{2,3},{3,4},{4,5},{5,6},{6,7},{7,8},{8,9},{9,10},{10,1... | collective-permute-start | bytes 786440 | tf_op jit(solution)/vmap(transpose(jvp()))/dot_general | solution.py:20
  1041.4 16.0 %collective-permute-start.5 = (f32[1,32,2048]{2,1,0:T(8,128)S(1)}, f32[1,32,2048]{2,1,0:T(8,128)S(1)}, u32[]{:S(2)}, u32[]{:S(2)}) collective-permute-start(f32[1,32,2048]{2,1,0:T(8,128)S(1)} %broadcast_select_fusion.27), channel_id=20, source_target_pairs={{0,15},{1,0},{2,1},{3,2},{4,3},{5,4},{6,5},{7,6},{8,7},{9,8},{10,9... | collective-permute-start | bytes 786440 | tf_op jit(solution)/vmap(transpose(jvp()))/dot_general | solution.py:20
  1071.1 16.1 %collective-permute-start.4 = (f32[1,32,2048]{2,1,0:T(8,128)S(1)}, f32[1,32,2048]{2,1,0:T(8,128)S(1)}, u32[]{:S(2)}, u32[]{:S(2)}) collective-permute-start(f32[1,32,2048]{2,1,0:T(8,128)S(1)} %broadcast_select_fusion.26), channel_id=21, source_target_pairs={{0,1},{1,2},{2,3},{3,4},{4,5},{5,6},{6,7},{7,8},{8,9},{9,10},{10,1... | collective-permute-start | bytes 786440 | tf_op jit(solution)/vmap(transpose(jvp()))/dot_general | solution.py:20
  1100.9 16.1 %collective-permute-start.4 = (f32[1,32,2048]{2,1,0:T(8,128)S(1)}, f32[1,32,2048]{2,1,0:T(8,128)S(1)}, u32[]{:S(2)}, u32[]{:S(2)}) collective-permute-start(f32[1,32,2048]{2,1,0:T(8,128)S(1)} %broadcast_select_fusion.26), channel_id=21, source_target_pairs={{0,1},{1,2},{2,3},{3,4},{4,5},{5,6},{6,7},{7,8},{8,9},{9,10},{10,1... | collective-permute-start | bytes 786440 | tf_op jit(solution)/vmap(transpose(jvp()))/dot_general | solution.py:20
  1101.0 16.0 %collective-permute-start.5 = (f32[1,32,2048]{2,1,0:T(8,128)S(1)}, f32[1,32,2048]{2,1,0:T(8,128)S(1)}, u32[]{:S(2)}, u32[]{:S(2)}) collective-permute-start(f32[1,32,2048]{2,1,0:T(8,128)S(1)} %broadcast_select_fusion.27), channel_id=20, source_target_pairs={{0,15},{1,0},{2,1},{3,2},{4,3},{5,4},{6,5},{7,6},{8,7},{9,8},{10,9... | collective-permute-start | bytes 786440 | tf_op jit(solution)/vmap(transpose(jvp()))/dot_general | solution.py:20
  1130.7 16.1 %collective-permute-start.4 = (f32[1,32,2048]{2,1,0:T(8,128)S(1)}, f32[1,32,2048]{2,1,0:T(8,128)S(1)}, u32[]{:S(2)}, u32[]{:S(2)}) collective-permute-start(f32[1,32,2048]{2,1,0:T(8,128)S(1)} %broadcast_select_fusion.26), channel_id=21, source_target_pairs={{0,1},{1,2},{2,3},{3,4},{4,5},{5,6},{6,7},{7,8},{8,9},{9,10},{10,1... | collective-permute-start | bytes 786440 | tf_op jit(solution)/vmap(transpose(jvp()))/dot_general | solution.py:20
  (123 other events, 2472.5 us)
Sparse Core Ops, SparseCore 0:
  10.2 44.4 all-gather.29
  56.9 40.2 all-gather.31
  99.4 40.2 all-gather.33
  141.7 40.2 all-gather.37
  184.0 40.2 all-gather.39
  226.4 40.2 all-gather.35
where the time goes:
time: 1200 us; the launch traced here: 1190 us
  matrix products  591 us (49%)
  starting transfers between devices  218 us (18%)
  waiting for transfers between devices  149 us (12%)
  local copies, waits for them, and re-layouts  96.8 us (8%)
  other arithmetic  74.5 us (6%)
  loops' own time  49.1 us (4%)
  between operations  15 us (1%)
    dot_general x20, matrix products, layer(): gate = jnp.dot(a, w['w_gate'], preferred_element_type=jnp.float32)  254 us
    dot_general x20, matrix products, layer(): up = jnp.dot(a, w['w_up'], preferred_element_type=jnp.float32)  222 us
    dot_general x19, matrix products, matmul(): jnp.dot(a, w, preferred_element_type=jnp.float32).astype(jnp.bfloat16)  115 us
    squeeze x6, waiting for transfers between devices, stack(): h = layer(h, {name: w[number] for name, w in weights.items()})  103 us
    unnamed x69, local copies, waits for them, and re-layouts  76.7 us
    dot_general x34, starting transfers between devices, matmul(): jnp.dot(a, w, preferred_element_type=jnp.float32).astype(jnp.bfloat16)  73.4 us
    dot_general x34, starting transfers between devices, layer(): up = jnp.dot(a, w['w_up'], preferred_element_type=jnp.float32)  72.4 us
    dot_general x34, starting transfers between devices, layer(): gate = jnp.dot(a, w['w_gate'], preferred_element_type=jnp.float32)  72.2 us
  transfers between devices with their start and end apart: 108, of which 21 were waited for; matrix products, arithmetic and copies ran while one was open for 55% of the time, Pallas kernels for 0%

commit v1 on v0

v1 whole, which is shorter than its diff:
```python
import functools

import jax
import jax.numpy as jnp
from jax import lax
from jax.experimental import pallas as pl
from jax.experimental.pallas import tpu as pltpu
from jax.sharding import PartitionSpec as P

MESH = pl.DeviceIdType.MESH
Y, Z, C = 2, 4, 2
NJ = 4
NT = 4
NQ = 4
bf, f32 = jnp.bfloat16, jnp.float32


def mm(a, b):
    return jnp.dot(a, b, preferred_element_type=f32)


def sigmoid(v):
    return 0.5 * jnp.tanh(0.5 * v) + 0.5


def scale_of(wide):
    return lax.rsqrt(jnp.mean(wide * wide, -1, keepdims=True) + 1e-6)


def kernel(x, dy, wg, wu, wd, dx, owg, owu, owd, h1, G, W, A, AT, DO, DOT, ACC, ag, au, ad, act_s, dgu, wt, wdt,
           P1g, P1w, Q1g, Q1w, P2g, P2w, Q2g, Q2w, K1g, K1w, P3g, P3w, K2g, K2w, Q3g, Q3w, Og, Ow,
           own_sem, tile_sem, tile2_sem, ags, agr, rss, rsr, out_sem, outw_sem):
    L = wg.shape[0]
    T, D = A.shape
    H = act_s
    TM = T // NT
    SUB = TM // 2
    R = wg.shape[1]
    FR = wd.shape[1]
    FC = NJ * FR
    HC = FC // 2
    me = lax.axis_index("dp")
    y, z, c = me // (Z * C), (me // C) % Z, me % C

    def dp(yy, zz, cc):
        return {"dp": (yy * Z + zz) * C + cc}

    partner, ypeer = dp(y, z, 1 - c), dp(1 - y, z, c)

    def zx(k):
        hi, lo = z // 2, z % 2
        if k & 2:
            hi = 1 - hi
        if k & 1:
            lo = 1 - lo
        return hi * 2 + lo

    zpeer = [None] + [dp(y, zx(k), c) for k in (1, 2, 3)]
    jmap = lambda i: i + 1 - 2 * (i % 2)

    def remote(src, dst, ss, rs, dev):
        return pltpu.make_async_remote_copy(src_ref=src, dst_ref=dst, send_sem=ss, recv_sem=rs, device_id=dev, device_id_type=MESH)

    def li(u):
        return u // NJ, jmap(u % NJ)

    def own_copies(l):
        out = []
        for j in range(NJ):
            for g, w in enumerate((wg, wu)):
                for h in range(2):
                    out.append(pltpu.make_async_copy(
                        w.at[l, :, pl.ds(h * (FC * 2) + j * HC, HC)], G.at[l, j, g, y, z, c, :, pl.ds(h * HC, HC)],
                        own_sem.at[l, (j * 2 + g) * 2 + h]))
        out.append(pltpu.make_async_copy(wd.at[l], W.at[l, z, y, c], own_sem.at[l, NJ * 4]))
        return out

    def g_piece(u, zz):
        l, j = li(u)
        ref = G.at[l, j, :, y, zz, c]
        return ref

    def ag_z(u, k):
        l, j = li(u)
        ref = G.at[l, j, :, y, z, c]
        return remote(ref, ref, ags.at[u, k - 1], agr.at[u, k - 1], zpeer[k])

    def ag_z_in(u, k):
        l, j = li(u)
        ref = G.at[l, j, :, y, zx(k), c]
        return remote(ref, ref, ags.at[u, k - 1], agr.at[u, k - 1], zpeer[k])

    def ag_zw(u, k):
        l, j = li(u)
        ref = W.at[l, j, y, c]
        return remote(ref, ref, ags.at[u, 2 + k], agr.at[u, 3], zpeer[k])

    def ag_y(u, k):
        l, j = li(u)
        ref = G.at[l, j, :, y, zx(k), c]
        return remote(ref, ref, ags.at[u, 6 + k], agr.at[u, 4 + k], ypeer)

    def ag_y_in(u, k):
        l, j = li(u)
        ref = G.at[l, j, :, 1 - y, zx(k), c]
        return remote(ref, ref, ags.at[u, 6 + k], agr.at[u, 4 + k], ypeer)

    def ag_yw(u, yy):
        l, j = li(u)
        ref = W.at[l, j, yy, c]
        return remote(ref, ref, ags.at[u, 10], agr.at[u, 8], ypeer)

    def ag_p(u, cc):
        l, j = li(u)
        ref = G.at[l, j, :, :, :, cc]
        return remote(ref, ref, ags.at[u, 11], agr.at[u, 9], partner)

    def ag_pw(u, cc):
        l, j = li(u)
        ref = W.at[l, j, :, cc]
        return remote(ref, ref, ags.at[u, 12], agr.at[u, 10], partner)

    def R1(u):
        l, j = li(u)
        for k in (1, 2, 3):
            ag_z(u, k).start()
        ag_y(u, 0).start()

        @pl.when(z == j)
        def _():
            for k in (1, 2, 3):
                ag_zw(u, k).start()
            ag_yw(u, y).start()

    def E(u, k):
        l, j = li(u)
        ag_z_in(u, k).wait_recv()
        ag_y(u, k).start()

    def Ew(u):
        l, j = li(u)

        @pl.when(z != j)
        def _():
            ag_zw(u, 1).wait_recv()
            ag_yw(u, y).start()

    def E4(u):
        for k in range(4):
            ag_y_in(u, k).wait_recv()
        ag_yw(u, 1 - y).wait_recv()
        ag_p(u, c).start()
        ag_pw(u, c).start()

    def E5(u):
        ag_p(u, 1 - c).wait_recv()
        ag_pw(u, 1 - c).wait_recv()

    def ag_finish(u):
        l, j = li(u)
        for k in (1, 2, 3):
            ag_z(u, k).wait_send()
        for k in range(4):
            ag_y(u, k).wait_send()

        @pl.when(z == j)
        def _():
            for k in (1, 2, 3):
                ag_zw(u, k).wait_send()
        ag_yw(u, y).wait_send()
        ag_p(u, c).wait_send()
        ag_pw(u, c).wait_send()

    def vl(v):
        return L - 1 - v // NJ, jmap(v % NJ)

    def s1(v):
        b = v % 2
        return (remote(P1g, Q1g.at[b], rss.at[0], rsr.at[b, 0], partner), remote(P1w, Q1w.at[b], rss.at[1], rsr.at[b, 1], partner))

    def s2(v):
        b = v % 2
        return (remote(P2g, Q2g.at[b], rss.at[2], rsr.at[b, 2], ypeer), remote(P2w, Q2w.at[b], rss.at[3], rsr.at[b, 3], ypeer))

    def s3(v, k):
        b = v % 2
        return remote(P3g.at[k], Q3g.at[b, k - 1], rss.at[3 + k], rsr.at[b, 3 + k], zpeer[k])

    def s3w(v, k):
        b = v % 2
        return remote(P3w, Q3w.at[k - 1], rss.at[7], rsr.at[b, 6 + k], zpeer[k])

    def wrows(yy, cc):
        return pl.ds(pl.multiple_of((yy * C + cc) * FR, FR), FR)

    def S1(v):
        @pl.when(v > 0)
        def _():
            for d in s1(v - 1):
                d.wait_send()
        for g, acc in enumerate((ag, au)):
            P1g[g] = acc[:, :, 1 - c].astype(bf)
        ad[...] = ad[...].T
        for yy in range(Y):
            P1w[yy] = ad[wrows(yy, 1 - c), :].astype(bf)
        for d in s1(v):
            d.start()

    def A1S2(v):
        b = v % 2
        for d in s1(v):
            d.wait_recv()

        @pl.when(v > 0)
        def _():
            for d in s2(v - 1):
                d.wait_send()
        for g, acc in enumerate((ag, au)):
            K1g[g] = acc[y, :, c] + Q1g[b, g, y].astype(f32)
            P2g[g] = (acc[1 - y, :, c] + Q1g[b, g, 1 - y].astype(f32)).astype(bf)
        K1w[...] = ad[wrows(y, c), :] + Q1w[b, y].astype(f32)
        P2w[...] = (ad[wrows(1 - y, c), :] + Q1w[b, 1 - y].astype(f32)).astype(bf)
        for d in s2(v):
            d.start()

    def s3_sent(v):
        l, j = vl(v)
        for k in (1, 2, 3):
            s3(v, k).wait_send()

        @pl.when(z != j)
        def _():
            s3w(v, 1).wait_send()

    def A2S3(v):
        l, j = vl(v)
        b = v % 2
        for d in s2(v):
            d.wait_recv()

        @pl.when(v > 0)
        def _():
            s3_sent(v - 1)
        for k in range(4):
            t = K1g[:, zx(k)] + Q2g[b, :, zx(k)].astype(f32)
            if k == 0:
                K2g[...] = t
            else:
                P3g[k] = t.astype(bf)
                s3(v, k).start()
        t = K1w[...] + Q2w[b].astype(f32)
        K2w[...] = t
        P3w[...] = t.astype(bf)
        for k in (1, 2, 3):
            @pl.when(zx(k) == j)
            def _():
                s3w(v, k).start()

    def out_copies(v):
        l, j = vl(v)
        return [pltpu.make_async_copy(Og.at[g, :, pl.ds(h * HC, HC)], o.at[l, :, pl.ds(pl.multiple_of(h * (FC * 2) + j * HC, 128), HC)],
                                      out_sem.at[g * 2 + h]) for g, o in enumerate((owg, owu)) for h in range(2)]

    def outw(l):
        return pltpu.make_async_copy(Ow.at[l], owd.at[l], outw_sem.at[l])

    def A3(v):
        l, j = vl(v)
        b = v % 2
        for k in (1, 2, 3):
            s3(v, k).wait_recv()

        @pl.when(v > 0)
        def _():
            for d in out_copies(v - 1):
                d.wait()
        Og[...] = (K2g[...] + Q3g[b, 0].astype(f32) + Q3g[b, 1].astype(f32) + Q3g[b, 2].astype(f32)).astype(bf)
        for d in out_copies(v):
            d.start()

        @pl.when(z == j)
        def _():
            for k in (1, 2, 3):
                s3w(v, k).wait_recv()
            Ow[l] = (K2w[...] + Q3w[0].astype(f32) + Q3w[1].astype(f32) + Q3w[2].astype(f32)).astype(bf)
            outw(l).start()

    def rows_of(t, s=0, n=None):
        return pl.ds(t * TM + s * SUB, SUB if n is None else n)

    def weight(l, j, g):
        return G[l, j, g].reshape(D, FC)

    QS = TM // NQ

    def pieces(t, f):
        def body(q, _):
            f(pl.ds(pl.multiple_of(t * TM + q * QS, QS), QS), pl.ds(pl.multiple_of(q * QS, QS), QS))
            return 0
        lax.fori_loop(0, NQ, body, 0)

    def norm_rows(h, r):
        wide = h.astype(f32)
        a = (wide * scale_of(wide)).astype(bf)
        A[r, :] = a
        AT[:, r] = a.T

    def load(src, t, dst, sem):
        return pltpu.make_async_copy(src.at[pl.ds(t * TM, TM)], dst, sem)

    def f0_step(i, t):
        l, j = 0, jmap(i)
        for s in range(2):
            r = rows_of(t, s)
            gate = mm(A[r, :], weight(l, j, 0))
            up = mm(A[r, :], weight(l, j, 1))
            act = (gate * sigmoid(gate) * up).astype(bf)
            act_s[0, s * SUB:(s + 1) * SUB, :] = act
        w = W[l, j].reshape(FC, D)
        for s in range(2):
            r = rows_of(t, s)
            o = mm(act_s[0, s * SUB:(s + 1) * SUB, :], w)
            ACC[r, :] = ACC[r, :] + o

    def fwd(l, j, t):
        b = t % 2
        for s in range(2):
            r = rows_of(t, s)
            rs = slice(s * SUB, (s + 1) * SUB)
            gate = mm(A[r, :], weight(l, j, 0))
            up = mm(A[r, :], weight(l, j, 1))
            dact = mm(DO[r, :], wdt[...]).astype(bf).astype(f32)
            sig = sigmoid(gate)
            silu = gate * sig
            act_s[b, rs, :] = (silu * up).astype(bf)
            dgu[b, rs, FC:] = (dact * silu).astype(bf)
            dgu[b, rs, :FC] = (dact * up * (sig + silu * (1.0 - sig))).astype(bf)

    def bwd(l, j, t):
        b = t % 2
        r = rows_of(t, 0, TM)
        new_g = mm(AT[:, r], dgu[b, :, :FC])
        new_u = mm(AT[:, r], dgu[b, :, FC:])
        new_d = mm(DOT[:, r], act_s[b])
        if t == 0:
            ag[...] = new_g.reshape(ag.shape)
            au[...] = new_u.reshape(au.shape)
            ad[...] = new_d
        else:
            ag[...] += new_g.reshape(ag.shape)
            au[...] += new_u.reshape(au.shape)
            ad[...] += new_d
        for s in range(2):
            r = rows_of(t, s)
            ACC[r, :] += mm(dgu[b, s * SUB:(s + 1) * SUB, :], wt[...])

    for l in range(L):
        for d in own_copies(l):
            d.start()
    for t in range(NT):
        load(x, t, DO.at[pl.ds(t * TM, TM)], tile_sem.at[t]).start()
    for t in range(2):
        load(dy, t, H.at[t], tile2_sem.at[t]).start()
    barrier = pltpu.get_barrier_semaphore()
    peers = [partner, ypeer] + zpeer[1:]
    for dev in peers:
        pl.semaphore_signal(barrier, inc=1, device_id=dev, device_id_type=MESH)
    pl.semaphore_wait(barrier, len(peers))
    for d in own_copies(0):
        d.wait()
    for u in range(NJ):
        R1(u)
    for d in own_copies(1):
        d.wait()
    for t in range(NT):
        load(x, t, DO.at[pl.ds(t * TM, TM)], tile_sem.at[t]).wait()
        load(dy, t, H.at[t % 2], tile2_sem.at[t % 2]).wait()

        def first(r, q):
            norm_rows(DO[r, :], r)
            ACC[r, :] = jnp.zeros_like(ACC[r, :])
            DOT[:, r] = H[t % 2, q, :].T
        pieces(t, first)
        if t + 2 < NT:
            load(dy, t + 2, H.at[t % 2], tile2_sem.at[t % 2]).start()
        if t == 0:
            E(0, 1)
        if t == 1:
            E(0, 2)
        if t == 2:
            E(0, 3)
            Ew(0)
    E(1, 1)
    E(1, 2)
    E4(0)
    E(1, 3)
    Ew(1)

    def f0_chunk(i, _):
        E5(i)
        f0_step(i, 0)

        @pl.when(i < 2)
        def _():
            E(i + 2, 1)
            E(i + 2, 2)

        @pl.when(i == 2)
        def _():
            for u in range(NJ, 2 * NJ):
                R1(u)

        @pl.when(i == 3)
        def _():
            E(NJ, 1)
            E(NJ, 2)
        f0_step(i, 1)
        f0_step(i, 2)

        @pl.when(i < 3)
        def _():
            E4(i + 1)
        f0_step(i, 3)

        @pl.when(i < 2)
        def _():
            E(i + 2, 3)
            Ew(i + 2)

        @pl.when(i == 3)
        def _():
            E(NJ, 3)
            Ew(NJ)
        return 0

    lax.fori_loop(0, NJ, f0_chunk, 0)

    for t in range(NT):
        def second(r, q):
            h = DO[r, :] + ACC[r, :].astype(bf)
            DO[r, :] = h
            ACC[r, :] = jnp.zeros_like(ACC[r, :])
            norm_rows(h, r)
        pieces(t, second)
        pltpu.make_async_copy(DO.at[pl.ds(t * TM, TM)], h1.at[pl.ds(t * TM, TM)], tile_sem.at[t]).start()
    E4(NJ)
    for t in range(NT):
        pltpu.make_async_copy(DO.at[pl.ds(t * TM, TM)], h1.at[pl.ds(t * TM, TM)], tile_sem.at[t]).wait()
        load(dy, t, DO.at[pl.ds(t * TM, TM)], tile_sem.at[t]).start()
    for t in range(NT):
        load(dy, t, DO.at[pl.ds(t * TM, TM)], tile_sem.at[t]).wait()

    def layer_back(n, _):
        l = L - 1 - n

        def chunk(i, _):
            j = jmap(i)
            v = n * NJ + i
            u = NJ + i

            @pl.when(n == 0)
            def _():
                E5(u)
            wt[:FC] = weight(l, j, 0).T
            wt[FC:] = weight(l, j, 1).T
            wdt[...] = W[l, j].reshape(FC, D).T
            fwd(l, j, 0)

            @pl.when(v > 0)
            def _():
                A1S2(v - 1)
            bwd(l, j, 0)
            fwd(l, j, 1)

            @pl.when(v > 1)
            def _():
                A3(v - 2)

            @pl.when((n == 0) & (i < NJ - 1))
            def _():
                E(u + 1, 1)
                E(u + 1, 2)
                E(u + 1, 3)
                Ew(u + 1)
            bwd(l, j, 1)
            fwd(l, j, 2)

            @pl.when(v > 0)
            def _():
                A2S3(v - 1)
            bwd(l, j, 2)
            fwd(l, j, 3)

            @pl.when((n == 0) & (i < NJ - 1))
            def _():
                E4(u + 1)
            bwd(l, j, 3)
            S1(v)
            return 0

        lax.fori_loop(0, NJ, chunk, 0)

        def hload(t):
            return pltpu.make_async_copy(h1.at[pl.ds(t * TM, TM)], H.at[t % 2], tile2_sem.at[t % 2])

        def xload(t):
            return pltpu.make_async_copy(x.at[pl.ds(t * TM, TM)], H.at[t % 2], tile2_sem.at[t % 2])

        def start_h(t):
            @pl.when(n == 0)
            def _():
                hload(t).start()

            @pl.when(n == 1)
            def _():
                xload(t).start()

        start_h(0)
        start_h(1)
        for t in range(NT):
            xload(t).wait()
            def third(r, q):
                wide = H[t % 2, q, :].astype(f32)
                scale = scale_of(wide)
                g = ACC[r, :].astype(bf).astype(f32)
                m = jnp.mean(g * wide, -1, keepdims=True)
                back = (g * scale - wide * (scale * scale * scale * m)).astype(bf)
                o = DO[r, :] + back
                DO[r, :] = o
                ACC[r, :] = jnp.zeros_like(ACC[r, :])
                DOT[:, r] = o.T
            pieces(t, third)
            if t + 2 < NT:
                start_h(t + 2)

            @pl.when(n == 1)
            def _():
                pltpu.make_async_copy(DO.at[pl.ds(t * TM, TM)], dx.at[pl.ds(t * TM, TM)], tile_sem.at[t]).start()

        @pl.when(n == 0)
        def _():
            for t in range(2):
                xload(t).start()
            for t in range(NT):
                xload(t).wait()
                pieces(t, lambda r, q: norm_rows(H[t % 2, q, :], r))
                if t + 2 < NT:
                    xload(t + 2).start()
        return 0

    lax.fori_loop(0, L, layer_back, 0)
    last = L * NJ - 1
    A1S2(last)
    A3(last - 1)
    A2S3(last)
    A3(last)
    for u in range(L * NJ):
        ag_finish(u)
    for d in s1(last) + s2(last):
        d.wait_send()
    s3_sent(last)
    for d in out_copies(last):
        d.wait()
    for l in range(L):
        outw(l).wait()
    for t in range(NT):
        pltpu.make_async_copy(DO.at[pl.ds(t * TM, TM)], dx.at[pl.ds(t * TM, TM)], tile_sem.at[t]).wait()


def solution(mesh):
    def step(x, dy, wg, wu, wd):
        x, dy = x[0], dy[0]
        L, R, FF = wg.shape
        T, D = x.shape
        FR = wd.shape[1]
        FC = NJ * FR
        TM = T // NT
        V, S = pltpu.VMEM, pltpu.SemaphoreType.DMA
        scratch = [
            V((L, NJ, 2, Y, Z, C, R, FC), bf), V((L, NJ, Y, C, FR, D), bf),
            V((T, D), bf), V((D, T), bf), V((T, D), bf), V((D, T), bf), V((T, D), f32),
            V((Y, Z, C, R, FC), f32), V((Y, Z, C, R, FC), f32), V((D, FC), f32),
            V((2, TM, FC), bf), V((2, TM, 2 * FC), bf), V((2 * FC, D), bf), V((D, FC), bf),
            V((2, Y, Z, R, FC), bf), V((Y, FR, D), bf), V((2, 2, Y, Z, R, FC), bf), V((2, Y, FR, D), bf),
            V((2, Z, R, FC), bf), V((FR, D), bf), V((2, 2, Z, R, FC), bf), V((2, FR, D), bf),
            V((2, Z, R, FC), f32), V((FR, D), f32),
            V((4, 2, R, FC), bf), V((FR, D), bf), V((2, R, FC), f32), V((FR, D), f32),
            V((2, 3, 2, R, FC), bf), V((3, FR, D), bf), V((2, R, FC), bf), V((L, FR, D), bf),
            S((L, NJ * 4 + 1)), S((NT,)), S((2,)), S((L * NJ, 13)), S((L * NJ, 11)), S((8,)), S((2, 10)), S((4,)), S((L,)),
        ]
        any_ = pl.BlockSpec(memory_space=pl.ANY)
        dx, g, u, d, _ = pl.pallas_call(
            kernel,
            out_shape=[jax.ShapeDtypeStruct(s, bf) for s in ((T, D), wg.shape, wu.shape, wd.shape, (T, D))],
            in_specs=[any_] * 5,
            out_specs=[any_] * 5,
            scratch_shapes=scratch,
            compiler_params=pltpu.CompilerParams(collective_id=0, has_side_effects=True, vmem_limit_bytes=67043328),
            name="stack",
        )(x, dy, wg, wu, wd)
        return dx[None], g, u, d

    w = P(None, "dp", None)
    t = P(("rep", "dp"), None, None)
    o = P("rep", "dp", None)
    return jax.shard_map(step, mesh=mesh, in_specs=(t, t, w, w, w), out_specs=(t, o, o, o), check_vma=False)
```

time: 1200 us -> 294 us (0.24)
  matrix products: 591 us -> 0 us
  Pallas kernels: 0 us -> 287 us
  starting transfers between devices: 218 us -> 0 us
  waiting for transfers between devices: 149 us -> 0 us
  local copies, waits for them, and re-layouts: 96.8 us -> 6.66 us
  other arithmetic: 74.5 us -> 0 us
  loops' own time: 49.1 us -> 0 us
  between operations: 15 us -> 0.67 us
    dot_general x59 -> x0, matrix products: 591 us -> none  [the longest x20 254 us: layer(): gate = jnp.dot(a, w['w_gate'], preferred_element_type=jnp.float32)]
    pallas_call x0 -> x1, Pallas kernels: none -> 287 us  [step(): pl.pallas_call(kernel, out_shape=[jax.ShapeDtypeStruct(s, bf) for s in ((...]
    dot_general x102 -> x0, starting transfers between devices: 218 us -> none  [the longest x34 73.4 us: matmul(): jnp.dot(a, w, preferred_element_type=jnp.float32).astype(jnp.bfloat16)]
    squeeze x6 -> x0, waiting for transfers between devices: 103 us -> none  [stack(): h = layer(h, {name: w[number] for name, w in weights.items()})]
    unnamed x69 -> x10, local copies, waits for them, and re-layouts: 76.7 us -> 6.66 us
    another operation x6 -> x0, loops' own time: 49.1 us -> none  [the longest x2 16.8 us: layer(): gate = jnp.dot(a, w['w_gate'], preferred_element_type=jnp.float32)]
    dot_general x102 -> x0, waiting for transfers between devices: 44.4 us -> none  [the longest x34 37.5 us: matmul(): jnp.dot(a, w, preferred_element_type=jnp.float32).astype(jnp.bfloat16)]
    convert_element_type x2 -> x0, other arithmetic: 32.9 us -> none  [the longest x1 27.6 us: layer(): (jax.nn.silu(gate) * up).astype(jnp.bfloat16)]
  transfers between devices with their start and end apart: 108 -> 0, of which waited for: 21 -> 0; matrix products, arithmetic and copies ran while one was open for 55% -> 0% of each run, Pallas kernels for 0% -> 0%
where the time goes in v1:
time: 294 us
  Pallas kernels  287 us (98%)
  local copies, waits for them, and re-layouts  6.66 us (2%)
    pallas_call x1, Pallas kernels, step(): pl.pallas_call(kernel, out_shape=[jax.ShapeDtypeStruct(s, bf) for s in ((...  287 us
    unnamed x10, local copies, waits for them, and re-layouts  6.66 us

profile of v1, /device:TPU:0, one launch (start us, length us, event | category | flops | bytes accessed | tf_op | source)
XLA Modules:
  0.0 293.8 jit_solution(14534297043374148489)
XLA Ops:
  0.6 286.5 %stack.1 = (bf16[4096,512]{1,0:T(8,128)(2,1)}, bf16[2,32,2048]{2,1,0:T(8,128)(2,1)}, bf16[2,32,2048]{2,1,0:T(8,128)(2,1)}, bf16[2,128,512]{2,1,0:T(8,128)(2,1)}, bf16[4096,512]{1,0:T(8,128)(2,1)}) custom-call(bf16[4096,512]{1,0:T(8,128)(2,1)} %bitcast.3, bf16[4096,512]{1,0:T(8,128)(2,1)} %bitcast.4, bf16[2,32,2048]{2,1,0:T(8,128)(2,1)} %wg.1, ...), custom_call_target="tpu_custom_call" | custom-call | tf_op jit(solution)/shard_map/stack/pallas_call | solution.py:592
  287.2 0.0 copy-start.2
  287.2 0.0 copy-start.1
  287.2 0.0 copy-start
  287.2 4.5 %copy.13 = bf16[1,4096,512]{2,1,0:T(8,128)(2,1)} copy(bf16[1,4096,512]{2,1,0:T(8,128)(2,1)} %bitcast.5) | data formatting | bytes 8388608
  291.7 0.0 copy-done.2
  291.7 0.7 copy.14
  292.4 0.0 copy-done.1
  292.4 0.7 copy.15
  293.1 0.0 copy-done
  293.1 0.7 copy.16
Async XLA Ops:
  287.2 4.6 %copy-start.2 = (bf16[2,32,2048]{2,1,0:T(8,128)(2,1)S(1)}, bf16[2,32,2048]{2,1,0:T(8,128)(2,1)}, u32[]{:S(2)}) copy-start(bf16[2,32,2048]{2,1,0:T(8,128)(2,1)} %get-tuple-element.17) | copy-start | bytes 786436
  287.2 5.3 %copy-start.1 = (bf16[2,32,2048]{2,1,0:T(8,128)(2,1)S(1)}, bf16[2,32,2048]{2,1,0:T(8,128)(2,1)}, u32[]{:S(2)}) copy-start(bf16[2,32,2048]{2,1,0:T(8,128)(2,1)} %get-tuple-element.18) | copy-start | bytes 786436
  287.2 6.0 %copy-start = (bf16[2,128,512]{2,1,0:T(8,128)(2,1)S(1)}, bf16[2,128,512]{2,1,0:T(8,128)(2,1)}, u32[]{:S(2)}) copy-start(bf16[2,128,512]{2,1,0:T(8,128)(2,1)} %get-tuple-element.19) | copy-start | bytes 786436

commit v2 on v1

--- a/solution.py
+++ b/solution.py
@@ -27,9 +27,9 @@
     return lax.rsqrt(jnp.mean(wide * wide, -1, keepdims=True) + 1e-6)
 
 
-def kernel(x, dy, wg, wu, wd, dx, owg, owu, owd, h1, G, W, A, AT, DO, DOT, ACC, ag, au, ad, act_s, dgu, wt, wdt,
+def kernel(x, dy, wg, wu, wd, dx, owg, owu, owd, h1, a0, a0t, G, W, A, AT, DO, DOT, ACC, ag, au, ad, act_s, dgu, wt, wdt,
            P1g, P1w, Q1g, Q1w, P2g, P2w, Q2g, Q2w, K1g, K1w, P3g, P3w, K2g, K2w, Q3g, Q3w, Og, Ow,
-           own_sem, tile_sem, tile2_sem, ags, agr, rss, rsr, out_sem, outw_sem):
+           own_sem, tile_sem, tile2_sem, ags, agr, rss, rsr, out_sem, outw_sem, a0_sem):
     L = wg.shape[0]
     T, D = A.shape
     H = act_s
@@ -40,6 +40,8 @@
     FC = NJ * FR
     HC = FC // 2
     me = lax.axis_index("dp")
+    xi = lax.axis_index("rep")
+    xpeer = {"rep": 1 - xi}
     y, z, c = me // (Z * C), (me // C) % Z, me % C
 
     def dp(yy, zz, cc):
@@ -75,40 +77,40 @@
         out.append(pltpu.make_async_copy(wd.at[l], W.at[l, z, y, c], own_sem.at[l, NJ * 4]))
         return out
 
-    def g_piece(u, zz):
-        l, j = li(u)
-        ref = G.at[l, j, :, y, zz, c]
-        return ref
-
-    def ag_z(u, k):
-        l, j = li(u)
-        ref = G.at[l, j, :, y, z, c]
-        return remote(ref, ref, ags.at[u, k - 1], agr.at[u, k - 1], zpeer[k])
-
-    def ag_z_in(u, k):
-        l, j = li(u)
-        ref = G.at[l, j, :, y, zx(k), c]
-        return remote(ref, ref, ags.at[u, k - 1], agr.at[u, k - 1], zpeer[k])
+    def g_ref(u, yy, zz, xx=None):
+        l, j = li(u)
+        return G.at[l, j, xi if xx is None else xx, yy, zz, c]
+
+    def w_ref(u, yy, xx=None):
+        l, j = li(u)
+        return W.at[l, j, yy, c, pl.ds(pl.multiple_of((xi if xx is None else xx) * (FR // 2), FR // 2), FR // 2)]
+
+    def same(ref, u, ss, rs, dev):
+        return remote(ref, ref, ags.at[u, ss], agr.at[u, rs], dev)
+
+    def ag_z(u, k, zz):
+        return same(g_ref(u, y, zz), u, k - 1, k - 1, zpeer[k])
 
     def ag_zw(u, k):
-        l, j = li(u)
-        ref = W.at[l, j, y, c]
-        return remote(ref, ref, ags.at[u, 2 + k], agr.at[u, 3], zpeer[k])
-
-    def ag_y(u, k):
-        l, j = li(u)
-        ref = G.at[l, j, :, y, zx(k), c]
-        return remote(ref, ref, ags.at[u, 6 + k], agr.at[u, 4 + k], ypeer)
-
-    def ag_y_in(u, k):
-        l, j = li(u)
-        ref = G.at[l, j, :, 1 - y, zx(k), c]
-        return remote(ref, ref, ags.at[u, 6 + k], agr.at[u, 4 + k], ypeer)
+        return same(w_ref(u, y), u, 2 + k, 3, zpeer[k])
+
+    def ag_y(u, k, yy):
+        return same(g_ref(u, yy, zx(k)), u, 6 + k, 4 + k, ypeer)
 
     def ag_yw(u, yy):
-        l, j = li(u)
-        ref = W.at[l, j, yy, c]
-        return remote(ref, ref, ags.at[u, 10], agr.at[u, 8], ypeer)
+        return same(w_ref(u, yy), u, 10, 8, ypeer)
+
+    def ag_x(u, k, xx=None):
+        return same(g_ref(u, y, zx(k), xx), u, 12 + k, 10 + k, xpeer)
+
+    def ag_xy(u, k, xx=None):
+        return same(g_ref(u, 1 - y, zx(k), xx), u, 16 + k, 14 + k, xpeer)
+
+    def ag_xw(u, xx=None):
+        return same(w_ref(u, y, xx), u, 20, 18, xpeer)
+
+    def ag_xyw(u, xx=None):
+        return same(w_ref(u, 1 - y, xx), u, 21, 19, xpeer)
 
     def ag_p(u, cc):
         l, j = li(u)
@@ -123,8 +125,8 @@
     def R1(u):
         l, j = li(u)
         for k in (1, 2, 3):
-            ag_z(u, k).start()
-        ag_y(u, 0).start()
+            ag_z(u, k, z).start()
+        ag_y(u, 0, y).start()
 
         @pl.when(z == j)
         def _():
@@ -132,23 +134,40 @@
                 ag_zw(u, k).start()
             ag_yw(u, y).start()
 
-    def E(u, k):
-        l, j = li(u)
-        ag_z_in(u, k).wait_recv()
-        ag_y(u, k).start()
-
-    def Ew(u):
-        l, j = li(u)
+    def E(u):
+        l, j = li(u)
+        for k in (1, 2, 3):
+            ag_z(u, k, zx(k)).wait_recv()
+            ag_y(u, k, y).start()
+            ag_x(u, k).start()
+            if k == 1:
+                ag_y(u, 0, 1 - y).wait_recv()
+                ag_xy(u, 0).start()
 
         @pl.when(z != j)
         def _():
             ag_zw(u, 1).wait_recv()
             ag_yw(u, y).start()
+            ag_xw(u).start()
 
     def E4(u):
+        for k in (1, 2, 3):
+            ag_y(u, k, 1 - y).wait_recv()
+            ag_xy(u, k).start()
+        ag_yw(u, 1 - y).wait_recv()
+        ag_xyw(u).start()
+
+    def Ex(u):
+        l, j = li(u)
+        for k in (1, 2, 3):
+            ag_x(u, k, 1 - xi).wait_recv()
         for k in range(4):
-            ag_y_in(u, k).wait_recv()
-        ag_yw(u, 1 - y).wait_recv()
+            ag_xy(u, k, 1 - xi).wait_recv()
+        ag_xyw(u, 1 - xi).wait_recv()
+
+        @pl.when(z != j)
+        def _():
+            ag_xw(u, 1 - xi).wait_recv()
         ag_p(u, c).start()
         ag_pw(u, c).start()
 
@@ -159,15 +178,23 @@
     def ag_finish(u):
         l, j = li(u)
         for k in (1, 2, 3):
-            ag_z(u, k).wait_send()
+            ag_z(u, k, z).wait_send()
+            ag_x(u, k).wait_send()
         for k in range(4):
-            ag_y(u, k).wait_send()
+            ag_y(u, k, y).wait_send()
 
         @pl.when(z == j)
         def _():
             for k in (1, 2, 3):
                 ag_zw(u, k).wait_send()
+
+        @pl.when(z != j)
+        def _():
+            ag_xw(u).wait_send()
         ag_yw(u, y).wait_send()
+        for k in range(4):
+            ag_xy(u, k).wait_send()
+        ag_xyw(u).wait_send()
         ag_p(u, c).wait_send()
         ag_pw(u, c).wait_send()
 
@@ -235,8 +262,7 @@
     def A2S3(v):
         l, j = vl(v)
         b = v % 2
-        for d in s2(v):
-            d.wait_recv()
+        s2(v)[0].wait_recv()
 
         @pl.when(v > 0)
         def _():
@@ -248,6 +274,7 @@
             else:
                 P3g[k] = t.astype(bf)
                 s3(v, k).start()
+        s2(v)[1].wait_recv()
         t = K1w[...] + Q2w[b].astype(f32)
         K2w[...] = t
         P3w[...] = t.astype(bf)
@@ -307,6 +334,12 @@
 
     def load(src, t, dst, sem):
         return pltpu.make_async_copy(src.at[pl.ds(t * TM, TM)], dst, sem)
+
+    def a0_out():
+        return [pltpu.make_async_copy(A, a0, a0_sem.at[0]), pltpu.make_async_copy(AT, a0t, a0_sem.at[1])]
+
+    def a0_in():
+        return [pltpu.make_async_copy(a0, A, a0_sem.at[0]), pltpu.make_async_copy(a0t, AT, a0_sem.at[1])]
 
     def f0_step(i, t):
         l, j = 0, jmap(i)
@@ -350,9 +383,13 @@
             ag[...] += new_g.reshape(ag.shape)
             au[...] += new_u.reshape(au.shape)
             ad[...] += new_d
+        if t < NT - 1:
+            bwd_a(t)
+
+    def bwd_a(t):
         for s in range(2):
             r = rows_of(t, s)
-            ACC[r, :] += mm(dgu[b, s * SUB:(s + 1) * SUB, :], wt[...])
+            ACC[r, :] += mm(dgu[t % 2, s * SUB:(s + 1) * SUB, :], wt[...])
 
     for l in range(L):
         for d in own_copies(l):
@@ -362,14 +399,13 @@
     for t in range(2):
         load(dy, t, H.at[t], tile2_sem.at[t]).start()
     barrier = pltpu.get_barrier_semaphore()
-    peers = [partner, ypeer] + zpeer[1:]
+    peers = [partner, ypeer, xpeer] + zpeer[1:]
     for dev in peers:
         pl.semaphore_signal(barrier, inc=1, device_id=dev, device_id_type=MESH)
     pl.semaphore_wait(barrier, len(peers))
     for d in own_copies(0):
         d.wait()
-    for u in range(NJ):
-        R1(u)
+    R1(0)
     for d in own_copies(1):
         d.wait()
     for t in range(NT):
@@ -384,56 +420,33 @@
         if t + 2 < NT:
             load(dy, t + 2, H.at[t % 2], tile2_sem.at[t % 2]).start()
         if t == 0:
-            E(0, 1)
+            R1(1)
         if t == 1:
-            E(0, 2)
-        if t == 2:
-            E(0, 3)
-            Ew(0)
-    E(1, 1)
-    E(1, 2)
-    E4(0)
-    E(1, 3)
-    Ew(1)
+            E(0)
+            R1(2)
+        if t == 3:
+            E4(0)
+    for d in a0_out():
+        d.start()
+    E(1)
+    Ex(0)
+    E4(1)
 
     def f0_chunk(i, _):
         E5(i)
         f0_step(i, 0)
-
-        @pl.when(i < 2)
-        def _():
-            E(i + 2, 1)
-            E(i + 2, 2)
-
-        @pl.when(i == 2)
-        def _():
-            for u in range(NJ, 2 * NJ):
-                R1(u)
-
-        @pl.when(i == 3)
-        def _():
-            E(NJ, 1)
-            E(NJ, 2)
+        E(i + 2)
+        R1(i + 3)
         f0_step(i, 1)
         f0_step(i, 2)
-
-        @pl.when(i < 3)
-        def _():
-            E4(i + 1)
+        Ex(i + 1)
         f0_step(i, 3)
-
-        @pl.when(i < 2)
-        def _():
-            E(i + 2, 3)
-            Ew(i + 2)
-
-        @pl.when(i == 3)
-        def _():
-            E(NJ, 3)
-            Ew(NJ)
+        E4(i + 2)
         return 0
 
     lax.fori_loop(0, NJ, f0_chunk, 0)
+    for d in a0_out():
+        d.wait()
 
     for t in range(NT):
         def second(r, q):
@@ -443,7 +456,6 @@
             norm_rows(h, r)
         pieces(t, second)
         pltpu.make_async_copy(DO.at[pl.ds(t * TM, TM)], h1.at[pl.ds(t * TM, TM)], tile_sem.at[t]).start()
-    E4(NJ)
     for t in range(NT):
         pltpu.make_async_copy(DO.at[pl.ds(t * TM, TM)], h1.at[pl.ds(t * TM, TM)], tile_sem.at[t]).wait()
         load(dy, t, DO.at[pl.ds(t * TM, TM)], tile_sem.at[t]).start()
@@ -466,7 +478,7 @@
             wdt[...] = W[l, j].reshape(FC, D).T
             fwd(l, j, 0)
 
-            @pl.when(v > 0)
+            @pl.when(i > 0)
             def _():
                 A1S2(v - 1)
             bwd(l, j, 0)
@@ -476,12 +488,13 @@
             def _():
                 A3(v - 2)
 
-            @pl.when((n == 0) & (i < NJ - 1))
-            def _():
-                E(u + 1, 1)
-                E(u + 1, 2)
-                E(u + 1, 3)
-                Ew(u + 1)
+            @pl.when((n == 0) & (i == 0))
+            def _():
+                R1(2 * NJ - 1)
+
+            @pl.when((n == 0) & (i < NJ - 2))
+            def _():
+                E(u + 2)
             bwd(l, j, 1)
             fwd(l, j, 2)
 
@@ -491,11 +504,16 @@
             bwd(l, j, 2)
             fwd(l, j, 3)
 
+            @pl.when((n == 0) & (i < NJ - 2))
+            def _():
+                E4(u + 2)
+
             @pl.when((n == 0) & (i < NJ - 1))
             def _():
-                E4(u + 1)
+                Ex(u + 1)
             bwd(l, j, 3)
             S1(v)
+            bwd_a(3)
             return 0
 
         lax.fori_loop(0, NJ, chunk, 0)
@@ -517,6 +535,11 @@
 
         start_h(0)
         start_h(1)
+
+        @pl.when(n == 0)
+        def _():
+            for d in a0_in():
+                d.start()
         for t in range(NT):
             xload(t).wait()
             def third(r, q):
@@ -530,6 +553,8 @@
                 ACC[r, :] = jnp.zeros_like(ACC[r, :])
                 DOT[:, r] = o.T
             pieces(t, third)
+            if t == 0:
+                A1S2(n * NJ + NJ - 1)
             if t + 2 < NT:
                 start_h(t + 2)
 
@@ -539,18 +564,12 @@
 
         @pl.when(n == 0)
         def _():
-            for t in range(2):
-                xload(t).start()
-            for t in range(NT):
-                xload(t).wait()
-                pieces(t, lambda r, q: norm_rows(H[t % 2, q, :], r))
-                if t + 2 < NT:
-                    xload(t + 2).start()
+            for d in a0_in():
+                d.wait()
         return 0
 
     lax.fori_loop(0, L, layer_back, 0)
     last = L * NJ - 1
-    A1S2(last)
     A3(last - 1)
     A2S3(last)
     A3(last)
@@ -565,6 +584,23 @@
         outw(l).wait()
     for t in range(NT):
         pltpu.make_async_copy(DO.at[pl.ds(t * TM, TM)], dx.at[pl.ds(t * TM, TM)], tile_sem.at[t]).wait()
+
+
+def hand_over(tiles, rows, *refs):
+    src, dst, via, sem = refs[:4], refs[4:8], refs[8:12], refs[12]
+
+    def part(ref, k, t):
+        return ref[k].at[pl.ds(t * rows, rows)] if k == 0 else ref[k].at[t]
+
+    into = [pltpu.make_async_copy(part(src, k, t), part(via, k, t), sem.at[n]) for n, (k, t) in enumerate(tiles)]
+    out = [pltpu.make_async_copy(part(via, k, t), part(dst, k, t), sem.at[n]) for n, (k, t) in enumerate(tiles)]
+    for d in into:
+        d.start()
+    for a, b in zip(into, out):
+        a.wait()
+        b.start()
+    for d in out:
+        d.wait()
 
 
 def solution(mesh):
@@ -586,18 +622,30 @@
             V((2, Z, R, FC), f32), V((FR, D), f32),
             V((4, 2, R, FC), bf), V((FR, D), bf), V((2, R, FC), f32), V((FR, D), f32),
             V((2, 3, 2, R, FC), bf), V((3, FR, D), bf), V((2, R, FC), bf), V((L, FR, D), bf),
-            S((L, NJ * 4 + 1)), S((NT,)), S((2,)), S((L * NJ, 13)), S((L * NJ, 11)), S((8,)), S((2, 10)), S((4,)), S((L,)),
+            S((L, NJ * 4 + 1)), S((NT,)), S((2,)), S((L * NJ, 22)), S((L * NJ, 20)), S((8,)), S((2, 10)), S((4,)), S((L,)), S((2,)),
         ]
         any_ = pl.BlockSpec(memory_space=pl.ANY)
-        dx, g, u, d, _ = pl.pallas_call(
+        dx, g, u, d, *_ = pl.pallas_call(
             kernel,
-            out_shape=[jax.ShapeDtypeStruct(s, bf) for s in ((T, D), wg.shape, wu.shape, wd.shape, (T, D))],
+            out_shape=[jax.ShapeDtypeStruct(s, bf) for s in ((T, D), wg.shape, wu.shape, wd.shape, (T, D), (T, D), (D, T))],
             in_specs=[any_] * 5,
-            out_specs=[any_] * 5,
+            out_specs=[any_] * 7,
             scratch_shapes=scratch,
             compiler_params=pltpu.CompilerParams(collective_id=0, has_side_effects=True, vmem_limit_bytes=67043328),
             name="stack",
         )(x, dy, wg, wu, wd)
+        outs = (dx, g, u, d)
+        tiles = [(k, t) for k in (1, 2, 3) for t in range(L)] + [(0, t) for t in range(8)]
+        dx, g, u, d = pl.pallas_call(
+            functools.partial(hand_over, tiles, T // 8),
+            out_shape=[jax.ShapeDtypeStruct(t.shape, bf) for t in outs],
+            in_specs=[any_] * 4,
+            out_specs=[any_] * 4,
+            scratch_shapes=[V(t.shape, bf) for t in outs] + [S((len(tiles),))],
+            compiler_params=pltpu.CompilerParams(vmem_limit_bytes=67043328),
+            cost_estimate=pl.CostEstimate(flops=0, bytes_accessed=10 * 2**20, transcendentals=0),
+            name="hand_over",
+        )(*outs)
         return dx[None], g, u, d
 
     w = P(None, "dp", None)

time: 294 us -> 267 us (0.908); the launches traced: 294 us -> 264 us
  Pallas kernels: 287 us -> 263 us
  local copies, waits for them, and re-layouts: 6.66 us -> 0 us
    pallas_call x1, Pallas kernels: 287 us -> 258 us  [step(): pl.pallas_call(kernel, out_shape=[jax.ShapeDtypeStruct(s, bf) for s in ((...]
    unnamed x10 -> x0, local copies, waits for them, and re-layouts: 6.66 us -> none
    pallas_call x0 -> x1, Pallas kernels: none -> 4.63 us  [step(): pl.pallas_call(functools.partial(hand_over, tiles, T // 8), out_shape=[ja...]
where the time goes in v2:
time: 267 us; the launch traced here: 264 us
  Pallas kernels  263 us (99%)
    pallas_call x1, Pallas kernels, step(): pl.pallas_call(kernel, out_shape=[jax.ShapeDtypeStruct(s, bf) for s in ((...  258 us

profile of v2, /device:TPU:0, one launch (start us, length us, event | category | flops | bytes accessed | tf_op | source)
XLA Modules:
  0.0 263.9 jit_solution(6221489381110060056)
XLA Ops:
  0.6 258.4 %stack.1 = (bf16[4096,512]{1,0:T(8,128)(2,1)}, bf16[2,32,2048]{2,1,0:T(8,128)(2,1)}, bf16[2,32,2048]{2,1,0:T(8,128)(2,1)}, bf16[2,128,512]{2,1,0:T(8,128)(2,1)},...) custom-call(bf16[4096,512]{1,0:T(8,128)(2,1)} %bitcast.3, ...), custom_call_target="tpu_custom_call" | custom-call | tf_op jit(solution)/shard_map/stack/pallas_call | solution.py:628
  259.1 4.6 %hand_over.1 = (bf16[4096,512]{1,0:T(8,128)(2,1)}, bf16[2,32,2048]{2,1,0:T(8,128)(2,1)}, bf16[2,32,2048]{2,1,0:T(8,128)(2,1)}, bf16[2,128,512]{2,1,0:T(8,128)(2,1)}) custom-call(bf16[4096,512]{1,0:T(8,128)(2,1)} %get-tuple-element.12.refs_0_, bf16[2,32,2048]{2,1,0:T(8,128)(2,1)} %get-tuple-element.13.refs_1_, ...), custom_call_target="tpu_custom_call" | custom-call | bytes 10485760 | tf_op jit(solution)/shard_map/hand_over/pallas_call | solution.py:639

commit v3 on v2

--- a/solution.py
+++ b/solution.py
@@ -435,9 +435,9 @@
     def f0_chunk(i, _):
         E5(i)
         f0_step(i, 0)
-        E(i + 2)
         R1(i + 3)
         f0_step(i, 1)
+        E(i + 2)
         f0_step(i, 2)
         Ex(i + 1)
         f0_step(i, 3)
@@ -473,14 +473,14 @@
             @pl.when(n == 0)
             def _():
                 E5(u)
+            wdt[...] = W[l, j].reshape(FC, D).T
+            fwd(l, j, 0)
+
+            @pl.when(i > 0)
+            def _():
+                A1S2(v - 1)
             wt[:FC] = weight(l, j, 0).T
             wt[FC:] = weight(l, j, 1).T
-            wdt[...] = W[l, j].reshape(FC, D).T
-            fwd(l, j, 0)
-
-            @pl.when(i > 0)
-            def _():
-                A1S2(v - 1)
             bwd(l, j, 0)
             fwd(l, j, 1)
 
@@ -552,9 +552,9 @@
                 DO[r, :] = o
                 ACC[r, :] = jnp.zeros_like(ACC[r, :])
                 DOT[:, r] = o.T
-            pieces(t, third)
             if t == 0:
                 A1S2(n * NJ + NJ - 1)
+            pieces(t, third)
             if t + 2 < NT:
                 start_h(t + 2)
 
@@ -635,9 +635,9 @@
             name="stack",
         )(x, dy, wg, wu, wd)
         outs = (dx, g, u, d)
-        tiles = [(k, t) for k in (1, 2, 3) for t in range(L)] + [(0, t) for t in range(8)]
+        tiles = [(k, t) for k in (1, 2, 3) for t in range(L)] + [(0, t) for t in range(16)]
         dx, g, u, d = pl.pallas_call(
-            functools.partial(hand_over, tiles, T // 8),
+            functools.partial(hand_over, tiles, T // 16),
             out_shape=[jax.ShapeDtypeStruct(t.shape, bf) for t in outs],
             in_specs=[any_] * 4,
             out_specs=[any_] * 4,

time: 267 us -> 268 us (level)
  Pallas kernels: 263 us -> 267 us
    pallas_call x1, Pallas kernels: 258 us -> 262 us  [step(): pl.pallas_call(kernel, out_shape=[jax.ShapeDtypeStruct(s, bf) for s in ((...]
where the time goes in v3:
time: 268 us; the launch traced here: 267 us
  Pallas kernels  267 us (100%)
    pallas_call x1, Pallas kernels, step(): pl.pallas_call(kernel, out_shape=[jax.ShapeDtypeStruct(s, bf) for s in ((...  262 us

profile of v3, /device:TPU:0, one launch (start us, length us, event | category | flops | bytes accessed | tf_op | source)
XLA Modules:
  0.0 267.4 jit_solution(11281129133994433620)
XLA Ops:
  0.6 262.0 %stack.1 = (bf16[4096,512]{1,0:T(8,128)(2,1)}, bf16[2,32,2048]{2,1,0:T(8,128)(2,1)}, bf16[2,32,2048]{2,1,0:T(8,128)(2,1)}, bf16[2,128,512]{2,1,0:T(8,128)(2,1)},...) custom-call(bf16[4096,512]{1,0:T(8,128)(2,1)} %bitcast.3, ...), custom_call_target="tpu_custom_call" | custom-call | tf_op jit(solution)/shard_map/stack/pallas_call | solution.py:628
  262.6 4.6 %hand_over.1 = (bf16[4096,512]{1,0:T(8,128)(2,1)}, bf16[2,32,2048]{2,1,0:T(8,128)(2,1)}, bf16[2,32,2048]{2,1,0:T(8,128)(2,1)}, bf16[2,128,512]{2,1,0:T(8,128)(2,1)}) custom-call(bf16[4096,512]{1,0:T(8,128)(2,1)} %get-tuple-element.12.refs_0_, bf16[2,32,2048]{2,1,0:T(8,128)(2,1)} %get-tuple-element.13.refs_1_, ...), custom_call_target="tpu_custom_call" | custom-call | bytes 10485760 | tf_op jit(solution)/shard_map/hand_over/pallas_call | solution.py:639
